TPU v7x, 32 devices: a 4x4x1 block of a 4x4x8 slice. The times are simulated.
32 devices in a mesh: data: 1 (over z), model: 4 (over y), stage: 8 (over x, core).
Axes of the slice: x: 4, y: 4, z: 1, core: 2. Of those that a mesh axis runs over, the one named last changes fastest.
The devices are a block of a 4x4x8 slice.
Arguments:
- inputs: bfloat16 [12, 384, 1024], P('data')
- targets: bfloat16 [12, 384, 1024], P('data')
- w_in: bfloat16 [8, 1, 1024, 4096], P('stage', None, None, 'model')
- w_out: bfloat16 [8, 1, 4096, 1024], P('stage', None, 'model')
Outputs:
- output 1: float32 [8, 1, 1024, 4096], P(('data', 'stage'), None, None, 'model')
- output 2: float32 [8, 1, 4096, 1024], P(('data', 'stage'), None, 'model')
- output 3: float32 [1], P('data')
All inputs are finite; a program needn't handle non-finite values.
Results may differ from a plain program's by a relative error of at most 0.00463857.
Values are sent between devices in bfloat16 or wider.
A program may use at most 768 MiB of HBM per device.

v0:
```python
import jax
import jax.numpy as jnp
from jax import lax
from jax.sharding import PartitionSpec as P

GELU_COEF = 0.7978845608028654
CUBIC_COEF = 0.044715


def gelu_tanh(values):
    inner_arg = GELU_COEF * (values + CUBIC_COEF * values * values * values)
    return 0.5 * values * (1.0 + jnp.tanh(inner_arg))


def gelu_slope(values):
    tanh_val = jnp.tanh(GELU_COEF * (values + CUBIC_COEF * values * values * values))
    return 0.5 * (1.0 + tanh_val) + 0.5 * values * (1.0 - tanh_val * tanh_val) * GELU_COEF * (1.0 + 3.0 * CUBIC_COEF * values * values)


def solution(mesh):
    n_stage = mesh.shape["stage"]
    down_perm = [(src_pos, src_pos + 1) for src_pos in range(n_stage - 1)]
    up_perm = [(src_pos + 1, src_pos) for src_pos in range(n_stage - 1)]

    def stage_step(inputs, targets, w_in, w_out):
        num_micro, num_tokens, model_dim = inputs.shape
        layers_here = w_in.shape[1]
        w_in_loc = w_in[0]
        w_out_loc = w_out[0]
        stage_pos = lax.axis_index("stage")
        is_last = stage_pos == n_stage - 1
        num_ticks = num_micro + n_stage - 1
        grad_scale = 1.0 / (num_micro * num_tokens * model_dim)

        def fwd_tick(state_in, tick_num):
            recv_act, loss_sum = state_in
            mb_index = tick_num - stage_pos
            first_in = lax.dynamic_index_in_dim(inputs, jnp.clip(tick_num, 0, num_micro - 1), 0, keepdims=False)
            hidden = jnp.where(stage_pos == 0, first_in, recv_act)
            saved_in = []
            saved_pre = []
            saved_act = []
            for layer_pos in range(layers_here):
                pre_act = jnp.dot(hidden, w_in_loc[layer_pos], preferred_element_type=jnp.float32).astype(jnp.bfloat16)
                act_out = gelu_tanh(pre_act.astype(jnp.float32)).astype(jnp.bfloat16)
                part_sum = jnp.dot(act_out, w_out_loc[layer_pos], preferred_element_type=jnp.float32)
                saved_in.append(hidden)
                saved_pre.append(pre_act)
                saved_act.append(act_out)
                hidden = (hidden.astype(jnp.float32) + lax.psum(part_sum, "model")).astype(jnp.bfloat16)
            tgt_mb = lax.dynamic_index_in_dim(targets, jnp.clip(mb_index, 0, num_micro - 1), 0, keepdims=False)
            out_err = hidden.astype(jnp.float32) - tgt_mb.astype(jnp.float32)
            start_grad = (out_err * grad_scale).astype(jnp.bfloat16)
            keep_loss = is_last & (mb_index >= 0) & (mb_index < num_micro)
            loss_sum = loss_sum + jnp.where(keep_loss, 0.5 * jnp.sum(out_err * out_err), 0.0)
            sent_act = lax.ppermute(hidden, "stage", down_perm)
            return (sent_act, loss_sum), (jnp.stack(saved_in), jnp.stack(saved_pre), jnp.stack(saved_act), start_grad)

        fwd_init = (jnp.zeros((num_tokens, model_dim), jnp.bfloat16), jnp.zeros((), jnp.float32))
        (last_act, loss_sum), (all_in, all_pre, all_act, all_start) = lax.scan(fwd_tick, fwd_init, jnp.arange(num_ticks))

        def bwd_tick(state_in, tick_num):
            recv_grad, acc_in, acc_out = state_in
            mb_index = tick_num - (n_stage - 1 - stage_pos)
            is_valid = (mb_index >= 0) & (mb_index < num_micro)
            save_pos = jnp.clip(mb_index + stage_pos, 0, num_ticks - 1)
            start_here = lax.dynamic_index_in_dim(all_start, save_pos, 0, keepdims=False)
            grad_h = jnp.where(is_last, start_here, recv_grad)
            grad_h = jnp.where(is_valid, grad_h, jnp.zeros_like(grad_h))
            layer_in = lax.dynamic_index_in_dim(all_in, save_pos, 0, keepdims=False)
            layer_pre = lax.dynamic_index_in_dim(all_pre, save_pos, 0, keepdims=False)
            layer_act = lax.dynamic_index_in_dim(all_act, save_pos, 0, keepdims=False)
            new_in = list(acc_in)
            new_out = list(acc_out)
            for layer_pos in reversed(range(layers_here)):
                grad_act = jnp.einsum("bd,fd->bf", grad_h, w_out_loc[layer_pos], preferred_element_type=jnp.float32).astype(jnp.bfloat16)
                grad_pre = (gelu_slope(layer_pre[layer_pos].astype(jnp.float32)) * grad_act.astype(jnp.float32)).astype(jnp.bfloat16)
                new_out[layer_pos] = new_out[layer_pos] + jnp.einsum("bf,bd->fd", layer_act[layer_pos], grad_h, preferred_element_type=jnp.float32)
                new_in[layer_pos] = new_in[layer_pos] + jnp.einsum("bd,bf->df", layer_in[layer_pos], grad_pre, preferred_element_type=jnp.float32)
                part_sum = jnp.einsum("bf,df->bd", grad_pre, w_in_loc[layer_pos], preferred_element_type=jnp.float32)
                grad_h = (grad_h.astype(jnp.float32) + lax.psum(part_sum, "model")).astype(jnp.bfloat16)
            sent_grad = lax.ppermute(grad_h, "stage", up_perm)
            return (sent_grad, tuple(new_in), tuple(new_out)), None

        zeros_in = tuple(jnp.zeros(w_in_loc.shape[1:], jnp.float32) for layer_pos in range(layers_here))
        zeros_out = tuple(jnp.zeros(w_out_loc.shape[1:], jnp.float32) for layer_pos in range(layers_here))
        bwd_init = (jnp.zeros((num_tokens, model_dim), jnp.bfloat16), zeros_in, zeros_out)
        (first_grad, acc_in, acc_out), unused_ys = lax.scan(bwd_tick, bwd_init, jnp.arange(num_ticks))
        loss_out = jnp.reshape(lax.psum(loss_sum, "stage") * grad_scale, (1,))
        return jnp.stack(acc_in)[None], jnp.stack(acc_out)[None], loss_out

    return jax.shard_map(
        stage_step,
        mesh=mesh,
        in_specs=(P("data", None, None), P("data", None, None), P("stage", None, None, "model"), P("stage", None, "model", None)),
        out_specs=(P(("data", "stage"), None, None, "model"), P(("data", "stage"), None, "model", None), P("data")),
        check_vma=False,
    )
```

profile of v0, /device:TPU:102, one launch (start us, length us, event | category | flops | bytes accessed | tf_op | source)
XLA Modules:
  0.0 2668.5 jit_solution(2883848733194481678)
XLA Ops:
  7.3 1339.6 %while.37 = (s32[]{:T(128)}, bf16[384,1024]{1,0:T(8,128)(2,1)S(1)}, f32[]{:T(128)}, bf16[19,1,384,1024]{3,2,1,0:T(8,128)(2,1)}, bf16[19,1,384,1024]{3,2,1,0:T(8,...) while((s32[]{:T(128)}, bf16[384,1024]{1,0:T(8,128)(2,1)S(1)}, ...), condition=%wide.region_3.4_spmd, body=%wide.region_0.3_spmd.sunk | while | flops 1624768512 | bytes 48499160 | solution.py:60
  16.6 47.6 %all-reduce.3.cloned.1.call-done = f32[384,1024]{1,0:T(8,128)} async-done(((f32[384,1024]{1,0:T(8,128)}), f32[384,1024]{1,0:T(8,128)}) %all-reduce.3.cloned.1.call-update) | async-done | bytes 1572880 | tf_op jit(solution)/shard_map/while/body/eval_jaxpr/psum | solution.py:50
  230.3 44.9 %all-reduce.3.cloned.1.call-done = f32[384,1024]{1,0:T(8,128)} async-done(((f32[384,1024]{1,0:T(8,128)}), f32[384,1024]{1,0:T(8,128)}) %all-reduce.3.cloned.1.call-update) | async-done | bytes 1572880 | tf_op jit(solution)/shard_map/while/body/eval_jaxpr/psum | solution.py:50
  300.7 44.9 %all-reduce.3.cloned.1.call-done = f32[384,1024]{1,0:T(8,128)} async-done(((f32[384,1024]{1,0:T(8,128)}), f32[384,1024]{1,0:T(8,128)}) %all-reduce.3.cloned.1.call-update) | async-done | bytes 1572880 | tf_op jit(solution)/shard_map/while/body/eval_jaxpr/psum | solution.py:50
  441.3 44.9 %all-reduce.3.cloned.1.call-done = f32[384,1024]{1,0:T(8,128)} async-done(((f32[384,1024]{1,0:T(8,128)}), f32[384,1024]{1,0:T(8,128)}) %all-reduce.3.cloned.1.call-update) | async-done | bytes 1572880 | tf_op jit(solution)/shard_map/while/body/eval_jaxpr/psum | solution.py:50
  722.7 44.9 %all-reduce.3.cloned.1.call-done = f32[384,1024]{1,0:T(8,128)} async-done(((f32[384,1024]{1,0:T(8,128)}), f32[384,1024]{1,0:T(8,128)}) %all-reduce.3.cloned.1.call-update) | async-done | bytes 1572880 | tf_op jit(solution)/shard_map/while/body/eval_jaxpr/psum | solution.py:50
  793.1 44.9 %all-reduce.3.cloned.1.call-done = f32[384,1024]{1,0:T(8,128)} async-done(((f32[384,1024]{1,0:T(8,128)}), f32[384,1024]{1,0:T(8,128)}) %all-reduce.3.cloned.1.call-update) | async-done | bytes 1572880 | tf_op jit(solution)/shard_map/while/body/eval_jaxpr/psum | solution.py:50
  863.5 44.9 %all-reduce.3.cloned.1.call-done = f32[384,1024]{1,0:T(8,128)} async-done(((f32[384,1024]{1,0:T(8,128)}), f32[384,1024]{1,0:T(8,128)}) %all-reduce.3.cloned.1.call-update) | async-done | bytes 1572880 | tf_op jit(solution)/shard_map/while/body/eval_jaxpr/psum | solution.py:50
  933.8 44.9 %all-reduce.3.cloned.1.call-done = f32[384,1024]{1,0:T(8,128)} async-done(((f32[384,1024]{1,0:T(8,128)}), f32[384,1024]{1,0:T(8,128)}) %all-reduce.3.cloned.1.call-update) | async-done | bytes 1572880 | tf_op jit(solution)/shard_map/while/body/eval_jaxpr/psum | solution.py:50
  1004.1 44.9 %all-reduce.3.cloned.1.call-done = f32[384,1024]{1,0:T(8,128)} async-done(((f32[384,1024]{1,0:T(8,128)}), f32[384,1024]{1,0:T(8,128)}) %all-reduce.3.cloned.1.call-update) | async-done | bytes 1572880 | tf_op jit(solution)/shard_map/while/body/eval_jaxpr/psum | solution.py:50
  1074.5 44.9 %all-reduce.3.cloned.1.call-done = f32[384,1024]{1,0:T(8,128)} async-done(((f32[384,1024]{1,0:T(8,128)}), f32[384,1024]{1,0:T(8,128)}) %all-reduce.3.cloned.1.call-update) | async-done | bytes 1572880 | tf_op jit(solution)/shard_map/while/body/eval_jaxpr/psum | solution.py:50
  1145.0 44.9 %all-reduce.3.cloned.1.call-done = f32[384,1024]{1,0:T(8,128)} async-done(((f32[384,1024]{1,0:T(8,128)}), f32[384,1024]{1,0:T(8,128)}) %all-reduce.3.cloned.1.call-update) | async-done | bytes 1572880 | tf_op jit(solution)/shard_map/while/body/eval_jaxpr/psum | solution.py:50
  1347.0 1301.2 %while.38 = (s32[]{:T(128)}, bf16[384,1024]{1,0:T(8,128)(2,1)S(1)}, f32[1024,1024]{1,0:T(8,128)}, f32[1024,1024]{1,0:T(8,128)}, s32[19]{0:T(128)S(1)}, /*index=5...) while((s32[]{:T(128)}, bf16[384,1024]{1,0:T(8,128)(2,1)S(1)}, ...), condition=%wide.region_6.7_spmd.clone, body=%wide.region_4.6_spmd.clone.sunk | while | flops 3236429824 | bytes 97255888 | solution.py:88
  1355.5 45.4 %all-reduce.5.cloned.1.call-done = f32[384,1024]{1,0:T(8,128)} async-done(((f32[384,1024]{1,0:T(8,128)}), f32[384,1024]{1,0:T(8,128)}) %all-reduce.5.cloned.1.call-update) | async-done | bytes 1572880 | tf_op jit(solution)/shard_map/while/body/eval_jaxpr/psum | solution.py:81
  1422.8 46.2 %all-reduce.5.cloned.1.call-done = f32[384,1024]{1,0:T(8,128)} async-done(((f32[384,1024]{1,0:T(8,128)}), f32[384,1024]{1,0:T(8,128)}) %all-reduce.5.cloned.1.call-update) | async-done | bytes 1572880 | tf_op jit(solution)/shard_map/while/body/eval_jaxpr/psum | solution.py:81
  1492.2 45.3 %all-reduce.5.cloned.1.call-done = f32[384,1024]{1,0:T(8,128)} async-done(((f32[384,1024]{1,0:T(8,128)}), f32[384,1024]{1,0:T(8,128)}) %all-reduce.5.cloned.1.call-update) | async-done | bytes 1572880 | tf_op jit(solution)/shard_map/while/body/eval_jaxpr/psum | solution.py:81
  1560.7 45.3 %all-reduce.5.cloned.1.call-done = f32[384,1024]{1,0:T(8,128)} async-done(((f32[384,1024]{1,0:T(8,128)}), f32[384,1024]{1,0:T(8,128)}) %all-reduce.5.cloned.1.call-update) | async-done | bytes 1572880 | tf_op jit(solution)/shard_map/while/body/eval_jaxpr/psum | solution.py:81
  1629.2 45.3 %all-reduce.5.cloned.1.call-done = f32[384,1024]{1,0:T(8,128)} async-done(((f32[384,1024]{1,0:T(8,128)}), f32[384,1024]{1,0:T(8,128)}) %all-reduce.5.cloned.1.call-update) | async-done | bytes 1572880 | tf_op jit(solution)/shard_map/while/body/eval_jaxpr/psum | solution.py:81
  1697.7 45.3 %all-reduce.5.cloned.1.call-done = f32[384,1024]{1,0:T(8,128)} async-done(((f32[384,1024]{1,0:T(8,128)}), f32[384,1024]{1,0:T(8,128)}) %all-reduce.5.cloned.1.call-update) | async-done | bytes 1572880 | tf_op jit(solution)/shard_map/while/body/eval_jaxpr/psum | solution.py:81
  1766.2 45.3 %all-reduce.5.cloned.1.call-done = f32[384,1024]{1,0:T(8,128)} async-done(((f32[384,1024]{1,0:T(8,128)}), f32[384,1024]{1,0:T(8,128)}) %all-reduce.5.cloned.1.call-update) | async-done | bytes 1572880 | tf_op jit(solution)/shard_map/while/body/eval_jaxpr/psum | solution.py:81
  1834.7 45.3 %all-reduce.5.cloned.1.call-done = f32[384,1024]{1,0:T(8,128)} async-done(((f32[384,1024]{1,0:T(8,128)}), f32[384,1024]{1,0:T(8,128)}) %all-reduce.5.cloned.1.call-update) | async-done | bytes 1572880 | tf_op jit(solution)/shard_map/while/body/eval_jaxpr/psum | solution.py:81
  1903.2 45.3 %all-reduce.5.cloned.1.call-done = f32[384,1024]{1,0:T(8,128)} async-done(((f32[384,1024]{1,0:T(8,128)}), f32[384,1024]{1,0:T(8,128)}) %all-reduce.5.cloned.1.call-update) | async-done | bytes 1572880 | tf_op jit(solution)/shard_map/while/body/eval_jaxpr/psum | solution.py:81
  1971.7 45.3 %all-reduce.5.cloned.1.call-done = f32[384,1024]{1,0:T(8,128)} async-done(((f32[384,1024]{1,0:T(8,128)}), f32[384,1024]{1,0:T(8,128)}) %all-reduce.5.cloned.1.call-update) | async-done | bytes 1572880 | tf_op jit(solution)/shard_map/while/body/eval_jaxpr/psum | solution.py:81
  2040.2 45.3 %all-reduce.5.cloned.1.call-done = f32[384,1024]{1,0:T(8,128)} async-done(((f32[384,1024]{1,0:T(8,128)}), f32[384,1024]{1,0:T(8,128)}) %all-reduce.5.cloned.1.call-update) | async-done | bytes 1572880 | tf_op jit(solution)/shard_map/while/body/eval_jaxpr/psum | solution.py:81
  2108.7 45.3 %all-reduce.5.cloned.1.call-done = f32[384,1024]{1,0:T(8,128)} async-done(((f32[384,1024]{1,0:T(8,128)}), f32[384,1024]{1,0:T(8,128)}) %all-reduce.5.cloned.1.call-update) | async-done | bytes 1572880 | tf_op jit(solution)/shard_map/while/body/eval_jaxpr/psum | solution.py:81
  2177.2 45.3 %all-reduce.5.cloned.1.call-done = f32[384,1024]{1,0:T(8,128)} async-done(((f32[384,1024]{1,0:T(8,128)}), f32[384,1024]{1,0:T(8,128)}) %all-reduce.5.cloned.1.call-update) | async-done | bytes 1572880 | tf_op jit(solution)/shard_map/while/body/eval_jaxpr/psum | solution.py:81
  2245.7 45.3 %all-reduce.5.cloned.1.call-done = f32[384,1024]{1,0:T(8,128)} async-done(((f32[384,1024]{1,0:T(8,128)}), f32[384,1024]{1,0:T(8,128)}) %all-reduce.5.cloned.1.call-update) | async-done | bytes 1572880 | tf_op jit(solution)/shard_map/while/body/eval_jaxpr/psum | solution.py:81
  2314.2 45.3 %all-reduce.5.cloned.1.call-done = f32[384,1024]{1,0:T(8,128)} async-done(((f32[384,1024]{1,0:T(8,128)}), f32[384,1024]{1,0:T(8,128)}) %all-reduce.5.cloned.1.call-update) | async-done | bytes 1572880 | tf_op jit(solution)/shard_map/while/body/eval_jaxpr/psum | solution.py:81
  2382.7 45.3 %all-reduce.5.cloned.1.call-done = f32[384,1024]{1,0:T(8,128)} async-done(((f32[384,1024]{1,0:T(8,128)}), f32[384,1024]{1,0:T(8,128)}) %all-reduce.5.cloned.1.call-update) | async-done | bytes 1572880 | tf_op jit(solution)/shard_map/while/body/eval_jaxpr/psum | solution.py:81
  2451.2 45.3 %all-reduce.5.cloned.1.call-done = f32[384,1024]{1,0:T(8,128)} async-done(((f32[384,1024]{1,0:T(8,128)}), f32[384,1024]{1,0:T(8,128)}) %all-reduce.5.cloned.1.call-update) | async-done | bytes 1572880 | tf_op jit(solution)/shard_map/while/body/eval_jaxpr/psum | solution.py:81
  2519.7 45.3 %all-reduce.5.cloned.1.call-done = f32[384,1024]{1,0:T(8,128)} async-done(((f32[384,1024]{1,0:T(8,128)}), f32[384,1024]{1,0:T(8,128)}) %all-reduce.5.cloned.1.call-update) | async-done | bytes 1572880 | tf_op jit(solution)/shard_map/while/body/eval_jaxpr/psum | solution.py:81
  2588.1 45.3 %all-reduce.5.cloned.1.call-done = f32[384,1024]{1,0:T(8,128)} async-done(((f32[384,1024]{1,0:T(8,128)}), f32[384,1024]{1,0:T(8,128)}) %all-reduce.5.cloned.1.call-update) | async-done | bytes 1572880 | tf_op jit(solution)/shard_map/while/body/eval_jaxpr/psum | solution.py:81
  (646 shorter events, 1246.1 us)
Async XLA Ops:
  7.3 56.9 %all-reduce.3.cloned.1.call-start = ((), (), s32[]{:S(2)}) async-start(), calls=%async_computation | async-start | bytes 3145728 | tf_op jit(solution)/shard_map/while/body/eval_jaxpr/psum | solution.py:50
  80.5 54.0 %all-reduce.3.cloned.1.call-start = ((), (), s32[]{:S(2)}) async-start(), calls=%async_computation | async-start | bytes 3145728 | tf_op jit(solution)/shard_map/while/body/eval_jaxpr/psum | solution.py:50
  150.9 54.0 %all-reduce.3.cloned.1.call-start = ((), (), s32[]{:S(2)}) async-start(), calls=%async_computation | async-start | bytes 3145728 | tf_op jit(solution)/shard_map/while/body/eval_jaxpr/psum | solution.py:50
  221.2 54.0 %all-reduce.3.cloned.1.call-start = ((), (), s32[]{:S(2)}) async-start(), calls=%async_computation | async-start | bytes 3145728 | tf_op jit(solution)/shard_map/while/body/eval_jaxpr/psum | solution.py:50
  291.5 54.0 %all-reduce.3.cloned.1.call-start = ((), (), s32[]{:S(2)}) async-start(), calls=%async_computation | async-start | bytes 3145728 | tf_op jit(solution)/shard_map/while/body/eval_jaxpr/psum | solution.py:50
  361.9 54.0 %all-reduce.3.cloned.1.call-start = ((), (), s32[]{:S(2)}) async-start(), calls=%async_computation | async-start | bytes 3145728 | tf_op jit(solution)/shard_map/while/body/eval_jaxpr/psum | solution.py:50
  432.2 54.0 %all-reduce.3.cloned.1.call-start = ((), (), s32[]{:S(2)}) async-start(), calls=%async_computation | async-start | bytes 3145728 | tf_op jit(solution)/shard_map/while/body/eval_jaxpr/psum | solution.py:50
  502.5 54.0 %all-reduce.3.cloned.1.call-start = ((), (), s32[]{:S(2)}) async-start(), calls=%async_computation | async-start | bytes 3145728 | tf_op jit(solution)/shard_map/while/body/eval_jaxpr/psum | solution.py:50
  572.8 54.0 %all-reduce.3.cloned.1.call-start = ((), (), s32[]{:S(2)}) async-start(), calls=%async_computation | async-start | bytes 3145728 | tf_op jit(solution)/shard_map/while/body/eval_jaxpr/psum | solution.py:50
  643.1 54.0 %all-reduce.3.cloned.1.call-start = ((), (), s32[]{:S(2)}) async-start(), calls=%async_computation | async-start | bytes 3145728 | tf_op jit(solution)/shard_map/while/body/eval_jaxpr/psum | solution.py:50
  713.5 54.1 %all-reduce.3.cloned.1.call-start = ((), (), s32[]{:S(2)}) async-start(), calls=%async_computation | async-start | bytes 3145728 | tf_op jit(solution)/shard_map/while/body/eval_jaxpr/psum | solution.py:50
  783.9 54.1 %all-reduce.3.cloned.1.call-start = ((), (), s32[]{:S(2)}) async-start(), calls=%async_computation | async-start | bytes 3145728 | tf_op jit(solution)/shard_map/while/body/eval_jaxpr/psum | solution.py:50
  854.3 54.0 %all-reduce.3.cloned.1.call-start = ((), (), s32[]{:S(2)}) async-start(), calls=%async_computation | async-start | bytes 3145728 | tf_op jit(solution)/shard_map/while/body/eval_jaxpr/psum | solution.py:50
  924.7 54.0 %all-reduce.3.cloned.1.call-start = ((), (), s32[]{:S(2)}) async-start(), calls=%async_computation | async-start | bytes 3145728 | tf_op jit(solution)/shard_map/while/body/eval_jaxpr/psum | solution.py:50
  995.0 54.0 %all-reduce.3.cloned.1.call-start = ((), (), s32[]{:S(2)}) async-start(), calls=%async_computation | async-start | bytes 3145728 | tf_op jit(solution)/shard_map/while/body/eval_jaxpr/psum | solution.py:50
  1065.3 54.0 %all-reduce.3.cloned.1.call-start = ((), (), s32[]{:S(2)}) async-start(), calls=%async_computation | async-start | bytes 3145728 | tf_op jit(solution)/shard_map/while/body/eval_jaxpr/psum | solution.py:50
  1135.7 54.1 %all-reduce.3.cloned.1.call-start = ((), (), s32[]{:S(2)}) async-start(), calls=%async_computation | async-start | bytes 3145728 | tf_op jit(solution)/shard_map/while/body/eval_jaxpr/psum | solution.py:50
  1206.1 54.0 %all-reduce.3.cloned.1.call-start = ((), (), s32[]{:S(2)}) async-start(), calls=%async_computation | async-start | bytes 3145728 | tf_op jit(solution)/shard_map/while/body/eval_jaxpr/psum | solution.py:50
  1276.5 54.0 %all-reduce.3.cloned.1.call-start = ((), (), s32[]{:S(2)}) async-start(), calls=%async_computation | async-start | bytes 3145728 | tf_op jit(solution)/shard_map/while/body/eval_jaxpr/psum | solution.py:50
  1347.0 53.9 %all-reduce.5.cloned.1.call-start = ((), (), s32[]{:S(2)}) async-start(), calls=%async_computation.1 | async-start | bytes 3145728 | tf_op jit(solution)/shard_map/while/body/eval_jaxpr/psum | solution.py:81
  1414.4 54.6 %all-reduce.5.cloned.1.call-start = ((), (), s32[]{:S(2)}) async-start(), calls=%async_computation.1 | async-start | bytes 3145728 | tf_op jit(solution)/shard_map/while/body/eval_jaxpr/psum | solution.py:81
  1552.2 53.7 %all-reduce.5.cloned.1.call-start = ((), (), s32[]{:S(2)}) async-start(), calls=%async_computation.1 | async-start | bytes 3145728 | tf_op jit(solution)/shard_map/while/body/eval_jaxpr/psum | solution.py:81
  1620.7 53.7 %all-reduce.5.cloned.1.call-start = ((), (), s32[]{:S(2)}) async-start(), calls=%async_computation.1 | async-start | bytes 3145728 | tf_op jit(solution)/shard_map/while/body/eval_jaxpr/psum | solution.py:81
  1689.2 53.7 %all-reduce.5.cloned.1.call-start = ((), (), s32[]{:S(2)}) async-start(), calls=%async_computation.1 | async-start | bytes 3145728 | tf_op jit(solution)/shard_map/while/body/eval_jaxpr/psum | solution.py:81
  1757.7 53.7 %all-reduce.5.cloned.1.call-start = ((), (), s32[]{:S(2)}) async-start(), calls=%async_computation.1 | async-start | bytes 3145728 | tf_op jit(solution)/shard_map/while/body/eval_jaxpr/psum | solution.py:81
  1826.2 53.7 %all-reduce.5.cloned.1.call-start = ((), (), s32[]{:S(2)}) async-start(), calls=%async_computation.1 | async-start | bytes 3145728 | tf_op jit(solution)/shard_map/while/body/eval_jaxpr/psum | solution.py:81
  1894.7 53.7 %all-reduce.5.cloned.1.call-start = ((), (), s32[]{:S(2)}) async-start(), calls=%async_computation.1 | async-start | bytes 3145728 | tf_op jit(solution)/shard_map/while/body/eval_jaxpr/psum | solution.py:81
  1963.2 53.7 %all-reduce.5.cloned.1.call-start = ((), (), s32[]{:S(2)}) async-start(), calls=%async_computation.1 | async-start | bytes 3145728 | tf_op jit(solution)/shard_map/while/body/eval_jaxpr/psum | solution.py:81
  2374.2 53.7 %all-reduce.5.cloned.1.call-start = ((), (), s32[]{:S(2)}) async-start(), calls=%async_computation.1 | async-start | bytes 3145728 | tf_op jit(solution)/shard_map/while/body/eval_jaxpr/psum | solution.py:81
  2442.7 53.7 %all-reduce.5.cloned.1.call-start = ((), (), s32[]{:S(2)}) async-start(), calls=%async_computation.1 | async-start | bytes 3145728 | tf_op jit(solution)/shard_map/while/body/eval_jaxpr/psum | solution.py:81
  2511.2 53.7 %all-reduce.5.cloned.1.call-start = ((), (), s32[]{:S(2)}) async-start(), calls=%async_computation.1 | async-start | bytes 3145728 | tf_op jit(solution)/shard_map/while/body/eval_jaxpr/psum | solution.py:81
  2579.7 53.7 %all-reduce.5.cloned.1.call-start = ((), (), s32[]{:S(2)}) async-start(), calls=%async_computation.1 | async-start | bytes 3145728 | tf_op jit(solution)/shard_map/while/body/eval_jaxpr/psum | solution.py:81
  (158 other events, 1136.5 us)
Sparse Core Ops, SparseCore 0:
  16.1 48.0 all-reduce.2
  89.2 45.2 all-reduce.2
  159.6 45.2 all-reduce.2
  229.9 45.2 all-reduce.2
  300.2 45.2 all-reduce.2
  370.6 45.2 all-reduce.2
  440.9 45.2 all-reduce.2
  511.2 45.2 all-reduce.2
  581.5 45.2 all-reduce.2
  651.8 45.2 all-reduce.2
  722.2 45.2 all-reduce.2
  792.6 45.2 all-reduce.2
  863.0 45.2 all-reduce.2
  933.3 45.2 all-reduce.2
  1003.7 45.2 all-reduce.2
  1074.0 45.2 all-reduce.2
  1144.5 45.2 all-reduce.2
  1214.9 45.2 all-reduce.2
  1285.3 45.2 all-reduce.2
  1355.6 45.2 all-reduce.4
  1422.9 45.9 all-reduce.4
  1560.8 45.1 all-reduce.4
  1629.3 45.1 all-reduce.4
  1697.8 45.1 all-reduce.4
  1766.3 45.1 all-reduce.4
  1834.8 45.1 all-reduce.4
  1903.3 45.1 all-reduce.4
  1971.8 45.1 all-reduce.4
  2040.3 45.1 all-reduce.4
  2108.8 45.1 all-reduce.4
  2177.3 45.1 all-reduce.4
  2245.8 45.1 all-reduce.4
  (6 shorter events, 270.5 us)
where the time goes:
time: 2680 us; the launch traced here: 2670 us
  waiting for transfers between devices  1890 us (71%)
  matrix products  356 us (13%)
  other arithmetic  204 us (8%)
  starting transfers between devices  79.4 us (3%)
  local copies, waits for them, and re-layouts  57.6 us (2%)
  loops' own time  49.1 us (2%)
    psum x19, waiting for transfers between devices, bwd_tick(): lax.psum(part_sum, 'model')  862 us
    psum x19, waiting for transfers between devices, fwd_tick(): lax.psum(part_sum, 'model')  855 us
    ppermute x19, waiting for transfers between devices, fwd_tick(): sent_act = lax.ppermute(hidden, 'stage', down_perm)  163 us
    dot_general x19, matrix products, bwd_tick(): jnp.einsum('bd,bf->df', layer_in[layer_pos], grad_pre, preferred_element_...  111 us
    dynamic_update_slice x38, other arithmetic, stage_step(): lax.scan(fwd_tick, fwd_init, jnp.arange(num_ticks))  106 us
    dot_general x19, matrix products, bwd_tick(): jnp.einsum('bd,fd->bf', grad_h, w_out_loc[layer_pos], preferred_element_t...  58 us
    dot_general x19, matrix products, bwd_tick(): jnp.einsum('bf,bd->fd', layer_act[layer_pos], grad_h, preferred_element_t...  55.8 us
  transfers between devices with their start and end apart: 76, of which 76 were waited for; matrix products, arithmetic and copies ran while one was open for 8% of the time, Pallas kernels for 0%

commit v1 on v0

v1 whole, which is shorter than its diff:
```python
import functools

import jax
import jax.numpy as jnp
from jax import lax
from jax.experimental import pallas as pl
from jax.experimental.pallas import tpu as pltpu
from jax.sharding import PartitionSpec as P

GELU_COEF = 0.7978845608028654
CUBIC_COEF = 0.044715
CHUNK = 128
MESH = pl.DeviceIdType.MESH


def gelu_tanh(values):
    inner_arg = GELU_COEF * (values + CUBIC_COEF * values * values * values)
    return 0.5 * values * (1.0 + jnp.tanh(inner_arg))


def gelu_slope(values):
    square = values * values
    tanh_val = jnp.tanh(GELU_COEF * (values + CUBIC_COEF * values * square))
    return 0.5 * (1.0 + tanh_val) + 0.5 * values * (1.0 - tanh_val * tanh_val) * GELU_COEF * (1.0 + 3.0 * CUBIC_COEF * square)


def dot_nn(lhs, rhs):
    return lax.dot_general(lhs, rhs, (((1,), (0,)), ((), ())), preferred_element_type=jnp.float32)


def dot_nt(lhs, rhs):
    return lax.dot_general(lhs, rhs, (((1,), (1,)), ((), ())), preferred_element_type=jnp.float32)


def chain_kernel(
    n_stage, n_model, n_chunk, grad_scale,
    in_hbm, tgt_hbm, w1_hbm, w2_hbm,
    x_all, e_all, loss_out,
    w1_v, w2_v, x_v, e_v, y_v, t_v, u_v, a_v, loss_acc, loss_parts, loss_tot,
    local_sem, w_send, w_recv,
    xp_send, xp_recv, ep_send, ep_recv,
    xg_send, xg_recv, eg_send, eg_recv, gl_sem,
    loss_send, loss_recv,
):
    stage = lax.axis_index("stage")
    me = lax.axis_index("model")
    last = n_stage - 1
    left = lax.rem(me + n_model - 1, n_model)
    right = lax.rem(me + 1, n_model)
    far = lax.rem(me + 2, n_model)
    is_first = stage == 0
    is_last = stage == last
    not_first = stage > 0
    not_last = stage < last
    ring_len = n_chunk
    dim, hid = w1_v.shape[1], w1_v.shape[2]
    half = dim // 2

    def remote(src, dst, send, recv, **where):
        return pltpu.make_async_remote_copy(
            src_ref=src, dst_ref=dst, send_sem=send, recv_sem=recv, device_id=where, device_id_type=MESH
        )

    barrier = pltpu.get_barrier_semaphore()
    for peer in (left, right, far):
        pl.semaphore_signal(barrier, inc=1, device_id={"model": peer}, device_id_type=MESH)

    @pl.when(not_first)
    def _():
        pl.semaphore_signal(barrier, inc=1, device_id={"stage": stage - 1}, device_id_type=MESH)

    @pl.when(not_last)
    def _():
        pl.semaphore_signal(barrier, inc=1, device_id={"stage": stage + 1}, device_id_type=MESH)

    num_peers = 5 - is_first.astype(jnp.int32) - is_last.astype(jnp.int32)
    pl.semaphore_wait(barrier, num_peers)

    def own_piece(w_hbm, w_v, idx, part, peer, slot):
        rows = pl.ds(part * half, half)
        return remote(w_hbm.at[rows], w_v.at[me, rows], w_send.at[idx, slot], w_recv.at[idx, slot], model=peer)

    def passed_piece(w_v, idx, owner, part, peer, slot):
        rows = pl.ds(part * half, half)
        return remote(w_v.at[owner, rows], w_v.at[owner, rows], w_send.at[idx, slot], w_recv.at[idx, slot], model=peer)

    weights = ((w1_hbm, w1_v, 0), (w2_hbm, w2_v, 1))
    def start_own(w_hbm, w_v, idx):
        own_piece(w_hbm, w_v, idx, 0, right, 0).start()
        own_piece(w_hbm, w_v, idx, 1, left, 3).start()
        own_piece(w_hbm, w_v, idx, 1, right, 1).start()
        own_piece(w_hbm, w_v, idx, 0, left, 2).start()

    def pass_on(w_hbm, w_v, idx):
        own_piece(w_hbm, w_v, idx, 0, right, 0).wait_recv()
        passed_piece(w_v, idx, left, 0, right, 4).start()
        own_piece(w_hbm, w_v, idx, 1, left, 3).wait_recv()
        passed_piece(w_v, idx, right, 1, left, 5).start()

    def finish_recv(w_hbm, w_v, idx):
        own_piece(w_hbm, w_v, idx, 1, right, 1).wait_recv()
        own_piece(w_hbm, w_v, idx, 0, left, 2).wait_recv()
        passed_piece(w_v, idx, left, 0, right, 4).wait_recv()
        passed_piece(w_v, idx, right, 1, left, 5).wait_recv()

    def finish_send(w_hbm, w_v, idx):
        own_piece(w_hbm, w_v, idx, 0, right, 0).wait_send()
        own_piece(w_hbm, w_v, idx, 1, left, 3).wait_send()
        own_piece(w_hbm, w_v, idx, 1, right, 1).wait_send()
        own_piece(w_hbm, w_v, idx, 0, left, 2).wait_send()
        passed_piece(w_v, idx, left, 0, right, 4).wait_send()
        passed_piece(w_v, idx, right, 1, left, 5).wait_send()

    start_own(*weights[0])
    own_copies = [pltpu.make_async_copy(w_hbm, w_v.at[me], local_sem.at[idx]) for w_hbm, w_v, idx in weights]
    for copy in own_copies:
        copy.start()
    mine = pl.ds(me * n_chunk, n_chunk)

    @pl.when(is_first)
    def _():
        load = pltpu.make_async_copy(in_hbm.at[mine], x_v, local_sem.at[2])
        load.start()
        load.wait()
        store = pltpu.make_async_copy(x_v, x_all.at[mine], local_sem.at[2])
        store.start()
        store.wait()
        for owner in (left, right, far):
            block = pl.ds(owner * n_chunk, n_chunk)
            load = pltpu.make_async_copy(in_hbm.at[block], t_v, local_sem.at[2])
            load.start()
            load.wait()
            store = pltpu.make_async_copy(t_v, x_all.at[block], local_sem.at[2])
            store.start()
            store.wait()

    @pl.when(is_last)
    def _():
        load = pltpu.make_async_copy(tgt_hbm.at[mine], t_v, local_sem.at[2])
        load.start()
        load.wait()
        loss_acc[...] = jnp.zeros_like(loss_acc)

    pass_on(*weights[0])
    start_own(*weights[1])
    pass_on(*weights[1])
    for copy in own_copies:
        copy.wait()
    finish_recv(*weights[0])
    finish_recv(*weights[1])

    def shared(src_v, dst_all, send, recv, pos, to_right):
        kind, peer = (0, right) if to_right else (1, left)
        return remote(src_v.at[pos], dst_all.at[me * n_chunk + pos], send.at[kind, pos], recv.at[kind, pos], model=peer)

    def passed(dst_all, send, recv, pos, to_right):
        owner, peer = (left, right) if to_right else (right, left)
        row = owner * n_chunk + pos
        return remote(dst_all.at[row], dst_all.at[row], send.at[2, pos], recv.at[2, pos], model=peer)

    def own_store(src_v, dst_all, idx, pos):
        return pltpu.make_async_copy(src_v.at[pos], dst_all.at[me * n_chunk + pos], gl_sem.at[idx, pos])

    def start_shared(src_v, dst_all, send, recv, idx, pos):
        shared(src_v, dst_all, send, recv, pos, True).start()
        shared(src_v, dst_all, send, recv, pos, False).start()
        own_store(src_v, dst_all, idx, pos).start()

    def relay(src_v, dst_all, send, recv, pos):
        @pl.when(lax.rem(pos, 2) == 0)
        def _():
            shared(src_v, dst_all, send, recv, pos, True).wait_recv()
            passed(dst_all, send, recv, pos, True).start()

        @pl.when(lax.rem(pos, 2) == 1)
        def _():
            shared(src_v, dst_all, send, recv, pos, False).wait_recv()
            passed(dst_all, send, recv, pos, False).start()

    def finish_gather(src_v, dst_all, send, recv, idx, pos):
        shared(src_v, dst_all, send, recv, pos, True).wait_send()
        shared(src_v, dst_all, send, recv, pos, False).wait_send()
        own_store(src_v, dst_all, idx, pos).wait()

        @pl.when(lax.rem(pos, 2) == 0)
        def _():
            shared(src_v, dst_all, send, recv, pos, False).wait_recv()
            passed(dst_all, send, recv, pos, True).wait()

        @pl.when(lax.rem(pos, 2) == 1)
        def _():
            shared(src_v, dst_all, send, recv, pos, True).wait_recv()
            passed(dst_all, send, recv, pos, False).wait()

    x_gather = (x_v, x_all, xg_send, xg_recv)
    e_gather = (e_v, e_all, eg_send, eg_recv)

    def act_copy(pos):
        return remote(y_v.at[pos], x_v.at[pos], xp_send.at[pos], xp_recv.at[pos], stage=stage + 1)

    def grad_copy(pos):
        return remote(y_v.at[pos], e_v.at[pos], ep_send.at[pos], ep_recv.at[pos], stage=stage - 1)

    @pl.loop(0, n_chunk)
    def _(pos):
        @pl.when(not_first)
        def _():
            act_copy(pos).wait_recv()
            start_shared(*x_gather, 0, pos)

        for part in range(n_model):
            cols = pl.ds(part * hid, hid)
            pre = dot_nn(x_v[pos], w1_v[part]).astype(jnp.bfloat16)
            u_v[pos, :, cols] = pre
            a_v[:, cols] = gelu_tanh(pre.astype(jnp.float32)).astype(jnp.bfloat16)
        branch = dot_nn(a_v[...], w2_v[...].reshape(n_model * hid, dim))
        y_v[pos] = (x_v[pos].astype(jnp.float32) + branch).astype(jnp.bfloat16)

        @pl.when(not_last)
        def _():
            act_copy(pos).start()

        @pl.when(is_last)
        def _():
            err = y_v[pos].astype(jnp.float32) - t_v[pos].astype(jnp.float32)
            e_v[pos] = (err * grad_scale).astype(jnp.bfloat16)
            loss_acc[...] += jnp.sum((err * err).reshape(-1, 8, dim), axis=0)

    def loss_share(kind, peer):
        return remote(loss_parts.at[0], loss_parts.at[1 + kind], loss_send.at[kind], loss_recv.at[kind], model=peer)

    @pl.when(is_last)
    def _():
        loss_parts[0] = jnp.full((8, 128), 0.5 * jnp.sum(loss_acc[...]), jnp.float32)

    @pl.loop(0, n_chunk)
    def _(pos):
        @pl.when(not_last)
        def _():
            grad_copy(pos).wait_recv()

        start_shared(*e_gather, 1, pos)

        @pl.when(not_last)
        def _():
            act_copy(pos).wait_send()

        @pl.when(not_first)
        def _():
            relay(*x_gather, pos)
            for part in range(n_model):
                cols = pl.ds(part * hid, hid)
                grad_act = dot_nt(e_v[pos], w2_v[part]).astype(jnp.bfloat16)
                slope = gelu_slope(u_v[pos, :, cols].astype(jnp.float32))
                a_v[:, cols] = (slope * grad_act.astype(jnp.float32)).astype(jnp.bfloat16)
            total = e_v[pos].astype(jnp.float32)
            branch = dot_nt(a_v[:, pl.ds(0, hid)], w1_v[0])
            for part in range(1, n_model):
                branch += dot_nt(a_v[:, pl.ds(part * hid, hid)], w1_v[part])
            y_v[pos] = (total + branch).astype(jnp.bfloat16)
            grad_copy(pos).start()

    def loss_down():
        return remote(loss_tot, loss_tot, loss_send.at[3], loss_recv.at[3], stage=stage - 1)

    @pl.when(is_last)
    def _():
        shares = [loss_share(kind, peer) for kind, peer in enumerate((left, right, far))]
        for copy in shares:
            copy.start()
        for copy in shares:
            copy.wait()
        pair_sum = (loss_parts[0] + loss_parts[3]) + (loss_parts[1] + loss_parts[2])
        loss_tot[...] = pair_sum * grad_scale

    @pl.when(not_last)
    def _():
        loss_down().wait_recv()

    @pl.when(not_first)
    def _():
        loss_down().start()

    for weight in weights:
        finish_send(*weight)

    @pl.loop(0, n_chunk)
    def _(pos):
        relay(*e_gather, pos)

    @pl.loop(0, n_chunk)
    def _(pos):
        @pl.when(not_first)
        def _():
            grad_copy(pos).wait_send()
            finish_gather(*x_gather, 0, pos)

        finish_gather(*e_gather, 1, pos)

    @pl.when(not_first)
    def _():
        loss_down().wait_send()

    loss_out[...] = loss_tot[...]


def solution(mesh):
    n_stage = mesh.shape["stage"]
    n_model = mesh.shape["model"]

    def stage_step(inputs, targets, w_in, w_out):
        num_micro, num_tokens, dim = inputs.shape
        hid = w_in.shape[3]
        w1, w2 = w_in[0, 0], w_out[0, 0]
        tokens = num_micro * num_tokens
        grad_scale = 1.0 / (tokens * dim)
        n_chunk = tokens // (n_model * CHUNK)
        chunked = (n_model * n_chunk, CHUNK, dim)
        any_spec = pl.BlockSpec(memory_space=pl.ANY)
        dma = pltpu.SemaphoreType.DMA
        block = pltpu.VMEM((n_chunk, CHUNK, dim), jnp.bfloat16)
        x_all, e_all, loss = pl.pallas_call(
            functools.partial(chain_kernel, n_stage, n_model, n_chunk, grad_scale),
            out_shape=(
                jax.ShapeDtypeStruct(chunked, jnp.bfloat16),
                jax.ShapeDtypeStruct(chunked, jnp.bfloat16),
                jax.ShapeDtypeStruct((8, 128), jnp.float32),
            ),
            in_specs=[any_spec] * 4,
            out_specs=(any_spec, any_spec, pl.BlockSpec(memory_space=pltpu.VMEM)),
            scratch_shapes=[
                pltpu.VMEM((n_model, dim, hid), jnp.bfloat16),
                pltpu.VMEM((n_model, hid, dim), jnp.bfloat16),
                block, block, block, block,
                pltpu.VMEM((n_chunk, CHUNK, n_model * hid), jnp.bfloat16),
                pltpu.VMEM((CHUNK, n_model * hid), jnp.bfloat16),
                pltpu.VMEM((8, dim), jnp.float32),
                pltpu.VMEM((4, 8, 128), jnp.float32),
                pltpu.VMEM((8, 128), jnp.float32),
                dma((3,)), dma((2, 6)), dma((2, 6)),
                dma((n_chunk,)), dma((n_chunk,)), dma((n_chunk,)), dma((n_chunk,)),
                dma((3, n_chunk)), dma((3, n_chunk)), dma((3, n_chunk)), dma((3, n_chunk)), dma((2, n_chunk)),
                dma((4,)), dma((4,)),
            ],
            compiler_params=pltpu.CompilerParams(
                collective_id=0, has_side_effects=True, vmem_limit_bytes=60 * 1024 * 1024
            ),
        )(inputs.reshape(chunked), targets.reshape(chunked), w1, w2)
        x_full = x_all.reshape(tokens, dim)
        e_full = e_all.reshape(tokens, dim)
        pre = dot_nn(x_full, w1).astype(jnp.bfloat16)
        act = gelu_tanh(pre.astype(jnp.float32)).astype(jnp.bfloat16)
        grad_act = dot_nt(e_full, w2).astype(jnp.bfloat16)
        grad_pre = (gelu_slope(pre.astype(jnp.float32)) * grad_act.astype(jnp.float32)).astype(jnp.bfloat16)
        contract_rows = (((0,), (0,)), ((), ()))
        grad_out = lax.dot_general(act, e_full, contract_rows, preferred_element_type=jnp.float32)
        grad_in = lax.dot_general(x_full, grad_pre, contract_rows, preferred_element_type=jnp.float32)
        return grad_in[None, None], grad_out[None, None], loss[0, :1]

    return jax.shard_map(
        stage_step,
        mesh=mesh,
        in_specs=(P("data", None, None), P("data", None, None), P("stage", None, None, "model"), P("stage", None, "model", None)),
        out_specs=(P(("data", "stage"), None, None, "model"), P(("data", "stage"), None, "model", None), P("data")),
        check_vma=False,
    )
```

time: 2680 us -> 433 us (0.16)
  the two profiles are of different devices: /device:TPU:102 before, /device:TPU:97 now
where the time goes in v1:
time: 433 us
  Pallas kernels  364 us (84%)
  matrix products  66.9 us (15%)
    pallas_call x1, Pallas kernels, stage_step(): pl.pallas_call(functools.partial(chain_kernel, n_stage, n_model, n_chunk,...  364 us
    dot_general x1, matrix products, stage_step(): lax.dot_general(x_full, grad_pre, contract_rows, preferred_element_type=j...  34.3 us
    dot_general x1, matrix products, stage_step(): lax.dot_general(act, e_full, contract_rows, preferred_element_type=jnp.fl...  16.9 us
    dot_general x1, matrix products, dot_nn(): lax.dot_general(lhs, rhs, (((1,), (0,)), ((), ())), preferred_element_typ...  15.8 us

profile of v1, /device:TPU:97, one launch (start us, length us, event | category | flops | bytes accessed | tf_op | source)
XLA Modules:
  0.0 432.7 jit_solution(15164280647080532297)
XLA Ops:
  0.6 0.0 copy-start
  0.6 363.9 %shard_map.67 = (bf16[36,128,1024]{2,1,0:T(8,128)(2,1)}, bf16[36,128,1024]{2,1,0:T(8,128)(2,1)}, f32[8,128]{1,0:T(8,128)}) custom-call(bf16[36,128,1024]{2,1,0:T(8,128)(2,1)} %bitcast.20, bf16[36,128,1024]{2,1,0:T(8,128)(2,1)} %bitcast.21, bf16[1024,1024]{1,0:T(8,128)(2,1)} %bitcast.22, bf16[1024,1024]{1,0:T(8,128)(2,1)} %bitcast.23), custom_call_target="tpu_custom_call" | custom-call | tf_op jit(solution)/shard_map/pallas_call | solution.py:322
  364.6 1.2 slice.3
  365.7 0.0 copy-done
  365.8 15.8 %convolution_convert_fusion.1 = bf16[4608,1024]{1,0:T(8,128)(2,1)} fusion(bf16[4608,1024]{1,0:T(8,128)(2,1)} %bitcast.26, bf16[1,1,1024,1024]{3,2,1,0:T(8,128)(2,1)S(1)} %copy-done), kind=kOutput, calls=%fused_computation.24 | convolution fusion | flops 9668395008 | bytes 20971520 | tf_op jit(solution)/shard_map/dot_general | solution.py:28
  381.5 34.3 %fusion.20 = f32[1,1,1024,1024]{3,2,1,0:T(8,128)} fusion(bf16[4608,1024]{1,0:T(8,128)(2,1)} %bitcast.27, bf16[4608,1024]{1,0:T(8,128)(2,1)} %convolution_convert_fusion.1, bf16[4608,1024]{1,0:T(8,128)(2,1)} %bitcast.24, bf16[1,1,1024,1024]{3,2,1,0:T(8,128)(2,1)} %param.7), kind=kOutput, calls=%fused_computation.27 | convolution fusion | flops 19426443264 | bytes 34603008 | tf_op jit(solution)/shard_map/dot_general | solution.py:357
  415.8 16.9 %fusion.23 = f32[1,1,1024,1024]{3,2,1,0:T(8,128)} fusion(bf16[4608,1024]{1,0:T(8,128)(2,1)} %bitcast.25, bf16[4608,1024]{1,0:T(8,128)(2,1)} %convolution_convert_fusion.1), kind=kOutput, calls=%fused_computation.28 | convolution fusion | flops 9710862336 | bytes 23068672 | tf_op jit(solution)/shard_map/dot_general | solution.py:356
Async XLA Ops:
  0.6 365.1 %copy-start = (bf16[1,1,1024,1024]{3,2,1,0:T(8,128)(2,1)S(1)}, bf16[1,1,1024,1024]{3,2,1,0:T(8,128)(2,1)}, u32[]{:S(2)}) copy-start(bf16[1,1,1024,1024]{3,2,1,0:T(8,128)(2,1)} %param.6) | copy-start | bytes 6291460

commit v2 on v1

v2 whole, which is shorter than its diff:
```python
import functools

import jax
import jax.numpy as jnp
from jax import lax
from jax.experimental import pallas as pl
from jax.experimental.pallas import tpu as pltpu
from jax.sharding import PartitionSpec as P

GELU_COEF = 0.7978845608028654
CUBIC_COEF = 0.044715
CHUNK = 128
MESH = pl.DeviceIdType.MESH


def gelu_tanh(values):
    inner_arg = GELU_COEF * (values + CUBIC_COEF * values * values * values)
    return 0.5 * values * (1.0 + jnp.tanh(inner_arg))


def gelu_slope(values):
    square = values * values
    tanh_val = jnp.tanh(GELU_COEF * (values + CUBIC_COEF * values * square))
    return 0.5 * (1.0 + tanh_val) + 0.5 * values * (1.0 - tanh_val * tanh_val) * GELU_COEF * (1.0 + 3.0 * CUBIC_COEF * square)


def dot_nn(lhs, rhs):
    return lax.dot_general(lhs, rhs, (((1,), (0,)), ((), ())), preferred_element_type=jnp.float32)


def dot_nt(lhs, rhs):
    return lax.dot_general(lhs, rhs, (((1,), (1,)), ((), ())), preferred_element_type=jnp.float32)


def dot_tn(lhs, rhs):
    return lax.dot_general(lhs, rhs, (((0,), (0,)), ((), ())), preferred_element_type=jnp.float32)


def step_kernel(
    n_stage, n_model, n_chunk, grad_scale,
    in_hbm, tgt_hbm, w1_hbm, w2_hbm,
    dw1, dw2, loss_out,
    w1_v, w2_v, x_v, e_v, yf_v, yb_v, u_v, a_v, du_v, da_v, loss_acc, loss_parts, loss_tot,
    local_sem, w_send, w_recv,
    xp_send, xp_recv, ep_send, ep_recv,
    xg_send, xg_recv, eg_send, eg_recv,
    loss_send, loss_recv,
):
    stage = lax.axis_index("stage")
    me = lax.axis_index("model")
    last = n_stage - 1
    left = lax.rem(me + n_model - 1, n_model)
    right = lax.rem(me + 1, n_model)
    far = lax.rem(me + 2, n_model)
    is_first = stage == 0
    is_last = stage == last
    not_first = stage > 0
    not_last = stage < last
    dim, hid = w1_v.shape[1], w1_v.shape[2]
    half = dim // 2
    rows_all = n_model * CHUNK

    def remote(src, dst, send, recv, **where):
        return pltpu.make_async_remote_copy(
            src_ref=src, dst_ref=dst, send_sem=send, recv_sem=recv, device_id=where, device_id_type=MESH
        )

    barrier = pltpu.get_barrier_semaphore()
    for peer in (left, right, far):
        pl.semaphore_signal(barrier, inc=1, device_id={"model": peer}, device_id_type=MESH)

    @pl.when(not_first)
    def _():
        pl.semaphore_signal(barrier, inc=1, device_id={"stage": stage - 1}, device_id_type=MESH)

    @pl.when(not_last)
    def _():
        pl.semaphore_signal(barrier, inc=1, device_id={"stage": stage + 1}, device_id_type=MESH)

    num_peers = 5 - is_first.astype(jnp.int32) - is_last.astype(jnp.int32)
    pl.semaphore_wait(barrier, num_peers)

    def own_piece(w_hbm, w_v, idx, part, peer, slot):
        rows = pl.ds(part * half, half)
        return remote(w_hbm.at[rows], w_v.at[me, rows], w_send.at[idx, slot], w_recv.at[idx, slot], model=peer)

    def passed_piece(w_v, idx, owner, part, peer, slot):
        rows = pl.ds(part * half, half)
        return remote(w_v.at[owner, rows], w_v.at[owner, rows], w_send.at[idx, slot], w_recv.at[idx, slot], model=peer)

    weights = ((w1_hbm, w1_v, 0), (w2_hbm, w2_v, 1))
    def start_own(w_hbm, w_v, idx):
        own_piece(w_hbm, w_v, idx, 0, right, 0).start()
        own_piece(w_hbm, w_v, idx, 1, left, 3).start()
        own_piece(w_hbm, w_v, idx, 1, right, 1).start()
        own_piece(w_hbm, w_v, idx, 0, left, 2).start()

    def pass_on(w_hbm, w_v, idx):
        own_piece(w_hbm, w_v, idx, 0, right, 0).wait_recv()
        passed_piece(w_v, idx, left, 0, right, 4).start()
        own_piece(w_hbm, w_v, idx, 1, left, 3).wait_recv()
        passed_piece(w_v, idx, right, 1, left, 5).start()

    def finish_recv(w_hbm, w_v, idx):
        own_piece(w_hbm, w_v, idx, 1, right, 1).wait_recv()
        own_piece(w_hbm, w_v, idx, 0, left, 2).wait_recv()
        passed_piece(w_v, idx, left, 0, right, 4).wait_recv()
        passed_piece(w_v, idx, right, 1, left, 5).wait_recv()

    def finish_send(w_hbm, w_v, idx):
        own_piece(w_hbm, w_v, idx, 0, right, 0).wait_send()
        own_piece(w_hbm, w_v, idx, 1, left, 3).wait_send()
        own_piece(w_hbm, w_v, idx, 1, right, 1).wait_send()
        own_piece(w_hbm, w_v, idx, 0, left, 2).wait_send()
        passed_piece(w_v, idx, left, 0, right, 4).wait_send()
        passed_piece(w_v, idx, right, 1, left, 5).wait_send()

    start_own(*weights[0])
    own_copies = [pltpu.make_async_copy(w_hbm, w_v.at[me], local_sem.at[idx]) for w_hbm, w_v, idx in weights]
    for copy in own_copies:
        copy.start()

    @pl.when(is_first)
    def _():
        loads = [pltpu.make_async_copy(in_hbm.at[owner], x_v.at[:, owner], local_sem.at[2 + owner]) for owner in range(n_model)]
        for load in loads:
            load.start()
        for load in loads:
            load.wait()

    @pl.when(is_last)
    def _():
        load = pltpu.make_async_copy(tgt_hbm.at[me], e_v.at[:, me], local_sem.at[2])
        load.start()
        load.wait()
        loss_acc[...] = jnp.zeros_like(loss_acc)

    dw1[...] = jnp.zeros_like(dw1)
    dw2[...] = jnp.zeros_like(dw2)

    pass_on(*weights[0])
    start_own(*weights[1])
    pass_on(*weights[1])
    for copy in own_copies:
        copy.wait()
    finish_recv(*weights[0])
    finish_recv(*weights[1])

    def shared(buf, send, recv, pos, to_right):
        kind, peer = (0, right) if to_right else (1, left)
        return remote(buf.at[pos, me], buf.at[pos, me], send.at[kind, pos], recv.at[kind, pos], model=peer)

    def passed(buf, send, recv, pos, to_right):
        owner, peer = (left, right) if to_right else (right, left)
        return remote(buf.at[pos, owner], buf.at[pos, owner], send.at[2, pos], recv.at[2, pos], model=peer)

    def start_shared(gather, pos):
        shared(*gather, pos, True).start()
        shared(*gather, pos, False).start()

    def by_parity(pos, even_fn, odd_fn):
        pl.when(lax.rem(pos, 2) == 0)(even_fn)
        pl.when(lax.rem(pos, 2) == 1)(odd_fn)

    def relay(gather, pos):
        def go(to_right):
            shared(*gather, pos, to_right).wait_recv()
            passed(*gather, pos, to_right).start()

        by_parity(pos, lambda: go(True), lambda: go(False))

    def arrived(gather, pos):
        def go(to_right):
            shared(*gather, pos, not to_right).wait_recv()
            passed(*gather, pos, to_right).wait_recv()

        by_parity(pos, lambda: go(True), lambda: go(False))

    def finish_gather(gather, pos):
        shared(*gather, pos, True).wait_send()
        shared(*gather, pos, False).wait_send()
        by_parity(pos, lambda: passed(*gather, pos, True).wait_send(), lambda: passed(*gather, pos, False).wait_send())

    x_gather = (x_v, xg_send, xg_recv)
    e_gather = (e_v, eg_send, eg_recv)

    def act_copy(pos):
        return remote(yf_v.at[lax.rem(pos, 2)], x_v.at[pos, me], xp_send.at[pos], xp_recv.at[pos], stage=stage + 1)

    def grad_copy(pos):
        return remote(yb_v.at[lax.rem(pos, 2)], e_v.at[pos, me], ep_send.at[pos], ep_recv.at[pos], stage=stage - 1)

    def forward(pos):
        @pl.when(not_first)
        def _():
            act_copy(pos).wait_recv()
            start_shared(x_gather, pos)

        @pl.when(not_last & (pos >= 2))
        def _():
            act_copy(pos - 2).wait_send()

        slot = lax.rem(pos, 2)
        for part in range(n_model):
            cols = pl.ds(part * hid, hid)
            pre = dot_nn(x_v[pos, me], w1_v[part]).astype(jnp.bfloat16)
            u_v[pos, :, cols] = pre
            a_v[:, cols] = gelu_tanh(pre.astype(jnp.float32)).astype(jnp.bfloat16)
        branch = dot_nn(a_v[...], w2_v[...].reshape(n_model * hid, dim))
        yf_v[slot] = (x_v[pos, me].astype(jnp.float32) + branch).astype(jnp.bfloat16)

        @pl.when(not_last)
        def _():
            act_copy(pos).start()

        @pl.when(is_last)
        def _():
            err = yf_v[slot].astype(jnp.float32) - e_v[pos, me].astype(jnp.float32)
            e_v[pos, me] = (err * grad_scale).astype(jnp.bfloat16)
            loss_acc[...] += jnp.sum((err * err).reshape(-1, 8, dim), axis=0)

    def backward(pos):
        @pl.when(not_last)
        def _():
            grad_copy(pos).wait_recv()

        start_shared(e_gather, pos)

        @pl.when(not_first)
        def _():
            @pl.when(pos >= 2)
            def _():
                grad_copy(pos - 2).wait_send()

            for part in range(n_model):
                cols = pl.ds(part * hid, hid)
                grad_act = dot_nt(e_v[pos, me], w2_v[part]).astype(jnp.bfloat16)
                slope = gelu_slope(u_v[pos, :, cols].astype(jnp.float32))
                a_v[:, cols] = (slope * grad_act.astype(jnp.float32)).astype(jnp.bfloat16)
            branch = dot_nt(a_v[:, pl.ds(0, hid)], w1_v[0])
            for part in range(1, n_model):
                branch += dot_nt(a_v[:, pl.ds(part * hid, hid)], w1_v[part])
            yb_v[lax.rem(pos, 2)] = (e_v[pos, me].astype(jnp.float32) + branch).astype(jnp.bfloat16)
            grad_copy(pos).start()

    def weight_grads(pos):
        @pl.when(not_first)
        def _():
            arrived(x_gather, pos)

        arrived(e_gather, pos)
        pre = dot_nn(x_v[pos].reshape(rows_all, dim), w1_v[me]).astype(jnp.bfloat16)
        du_v[...] = pre
        da_v[...] = gelu_tanh(pre.astype(jnp.float32)).astype(jnp.bfloat16)
        dw2[...] += dot_tn(da_v[...], e_v[pos].reshape(rows_all, dim))
        grad_act = dot_nt(e_v[pos].reshape(rows_all, dim), w2_v[me]).astype(jnp.bfloat16)
        slope = gelu_slope(du_v[...].astype(jnp.float32))
        da_v[...] = (slope * grad_act.astype(jnp.float32)).astype(jnp.bfloat16)
        dw1[...] += dot_tn(x_v[pos].reshape(rows_all, dim), da_v[...])

    def loss_share(kind, peer):
        return remote(loss_parts.at[0], loss_parts.at[1 + kind], loss_send.at[kind], loss_recv.at[kind], model=peer)

    def loss_down():
        return remote(loss_tot, loss_tot, loss_send.at[3], loss_recv.at[3], stage=stage - 1)

    warm = jnp.minimum(n_chunk, 1 + 3 * (last - stage)) - 1
    is_late = stage >= n_stage // 2
    relay_at = jnp.where(is_late, warm + n_chunk - 2, warm + 1)
    grads_at = jnp.where(is_late, warm + n_chunk, warm + 2)
    loss_at = jnp.where(is_late, grads_at, grads_at + n_chunk - 2)
    x_lag = 5

    def due(turn, start, fn):
        pos = turn - start
        pl.when((pos >= 0) & (pos < n_chunk))(lambda: fn(pos))

    @pl.loop(0, grads_at + n_chunk)
    def _(turn):
        due(turn, 0, forward)
        due(turn, warm, backward)

        @pl.when(not_first)
        def _():
            due(turn, x_lag, functools.partial(relay, x_gather))

        due(turn, relay_at, functools.partial(relay, e_gather))

        @pl.when(is_last & (turn == n_chunk - 1))
        def _():
            loss_parts[0] = jnp.full((8, 128), 0.5 * jnp.sum(loss_acc[...]), jnp.float32)

        @pl.when(turn == loss_at)
        def _():
            @pl.when(is_last)
            def _():
                shares = [loss_share(kind, peer) for kind, peer in enumerate((left, right, far))]
                for copy in shares:
                    copy.start()
                for copy in shares:
                    copy.wait()
                pair_sum = (loss_parts[0] + loss_parts[3]) + (loss_parts[1] + loss_parts[2])
                loss_tot[...] = pair_sum * grad_scale

            @pl.when(not_last)
            def _():
                loss_down().wait_recv()

            @pl.when(not_first)
            def _():
                loss_down().start()

        due(turn, grads_at, weight_grads)

    for weight in weights:
        finish_send(*weight)

    @pl.loop(0, n_chunk)
    def _(pos):
        @pl.when(not_first)
        def _():
            finish_gather(x_gather, pos)

        finish_gather(e_gather, pos)

    for pos in (n_chunk - 2, n_chunk - 1):
        @pl.when(not_last)
        def _():
            act_copy(pos).wait_send()

        @pl.when(not_first)
        def _():
            grad_copy(pos).wait_send()

    @pl.when(not_first)
    def _():
        loss_down().wait_send()

    loss_out[...] = loss_tot[...]


def solution(mesh):
    n_stage = mesh.shape["stage"]
    n_model = mesh.shape["model"]

    def stage_step(inputs, targets, w_in, w_out):
        num_micro, num_tokens, dim = inputs.shape
        hid = w_in.shape[3]
        w1, w2 = w_in[0, 0], w_out[0, 0]
        tokens = num_micro * num_tokens
        grad_scale = 1.0 / (tokens * dim)
        n_chunk = tokens // (n_model * CHUNK)
        by_owner = (n_model, n_chunk, CHUNK, dim)
        any_spec = pl.BlockSpec(memory_space=pl.ANY)
        vmem_spec = pl.BlockSpec(memory_space=pltpu.VMEM)
        dma = pltpu.SemaphoreType.DMA
        bf16, f32 = jnp.bfloat16, jnp.float32
        dw1, dw2, loss = pl.pallas_call(
            functools.partial(step_kernel, n_stage, n_model, n_chunk, grad_scale),
            out_shape=(
                jax.ShapeDtypeStruct((dim, hid), f32),
                jax.ShapeDtypeStruct((hid, dim), f32),
                jax.ShapeDtypeStruct((8, 128), f32),
            ),
            in_specs=[any_spec] * 4,
            out_specs=(vmem_spec, vmem_spec, vmem_spec),
            scratch_shapes=[
                pltpu.VMEM((n_model, dim, hid), bf16),
                pltpu.VMEM((n_model, hid, dim), bf16),
                pltpu.VMEM((n_chunk, n_model, CHUNK, dim), bf16),
                pltpu.VMEM((n_chunk, n_model, CHUNK, dim), bf16),
                pltpu.VMEM((2, CHUNK, dim), bf16),
                pltpu.VMEM((2, CHUNK, dim), bf16),
                pltpu.VMEM((n_chunk, CHUNK, n_model * hid), bf16),
                pltpu.VMEM((CHUNK, n_model * hid), bf16),
                pltpu.VMEM((n_model * CHUNK, hid), bf16),
                pltpu.VMEM((n_model * CHUNK, hid), bf16),
                pltpu.VMEM((8, dim), f32),
                pltpu.VMEM((4, 8, 128), f32),
                pltpu.VMEM((8, 128), f32),
                dma((2 + n_model,)), dma((2, 6)), dma((2, 6)),
                dma((n_chunk,)), dma((n_chunk,)), dma((n_chunk,)), dma((n_chunk,)),
                dma((3, n_chunk)), dma((3, n_chunk)), dma((3, n_chunk)), dma((3, n_chunk)),
                dma((4,)), dma((4,)),
            ],
            compiler_params=pltpu.CompilerParams(
                collective_id=0, has_side_effects=True, vmem_limit_bytes=67043328
            ),
        )(inputs.reshape(by_owner), targets.reshape(by_owner), w1, w2)
        return dw1[None, None], dw2[None, None], loss[0, :1]

    return jax.shard_map(
        stage_step,
        mesh=mesh,
        in_specs=(P("data", None, None), P("data", None, None), P("stage", None, None, "model"), P("stage", None, "model", None)),
        out_specs=(P(("data", "stage"), None, None, "model"), P(("data", "stage"), None, "model", None), P("data")),
        check_vma=False,
    )
```

time: 433 us -> 375 us (0.87)
  the two profiles are of different devices: /device:TPU:97 before, /device:TPU:102 now
where the time goes in v2:
time: 375 us; the launch traced here: 371 us
  Pallas kernels  362 us (97%)
  local copies, waits for them, and re-layouts  8.15 us (2%)
    pallas_call x1, Pallas kernels, stage_step(): pl.pallas_call(functools.partial(step_kernel, n_stage, n_model, n_chunk,...  362 us

profile of v2, /device:TPU:102, one launch (start us, length us, event | category | flops | bytes accessed | tf_op | source)
XLA Modules:
  0.0 371.2 jit_solution(10383757319033109407)
XLA Ops:
  0.6 362.4 %shard_map.67 = (f32[1024,1024]{1,0:T(8,128)}, f32[1024,1024]{1,0:T(8,128)}, f32[8,128]{1,0:T(8,128)}) custom-call(bf16[4,9,128,1024]{3,2,1,0:T(8,128)(2,1)} %bitcast.7, bf16[4,9,128,1024]{3,2,1,0:T(8,128)(2,1)} %bitcast.8, bf16[1024,1024]{1,0:T(8,128)(2,1)} %bitcast.11, bf16[1024,1024]{1,0:T(8,128)(2,1)} %bitcast.12), custom_call_target="tpu_custom_call" | custom-call | tf_op jit(solution)/shard_map/pallas_call | solution.py:358
  363.1 1.2 slice.3
  364.2 0.0 copy-start
  364.2 4.9 %copy.9 = f32[1,1,1024,1024]{3,2,1,0:T(8,128)} copy(f32[1,1,1024,1024]{3,2,1,0:T(8,128)} %bitcast.10) | data formatting | bytes 8388608
  369.2 0.0 copy-done
  369.2 2.0 copy.10
Async XLA Ops:
  364.2 4.9 %copy-start = (f32[1024,1024]{1,0:T(8,128)S(1)}, f32[1024,1024]{1,0:T(8,128)}, u32[]{:S(2)}) copy-start(f32[1024,1024]{1,0:T(8,128)} %get-tuple-element.7) | copy-start | bytes 12582916

commit v3 on v2

--- a/solution.py
+++ b/solution.py
@@ -176,42 +176,51 @@
 
         by_parity(pos, lambda: go(True), lambda: go(False))
 
-    def finish_gather(gather, pos):
+    def finish_shared(gather, pos):
         shared(*gather, pos, True).wait_send()
         shared(*gather, pos, False).wait_send()
+
+    def finish_passed(gather, pos):
         by_parity(pos, lambda: passed(*gather, pos, True).wait_send(), lambda: passed(*gather, pos, False).wait_send())
 
     x_gather = (x_v, xg_send, xg_recv)
     e_gather = (e_v, eg_send, eg_recv)
 
-    def act_copy(pos):
-        return remote(yf_v.at[lax.rem(pos, 2)], x_v.at[pos, me], xp_send.at[pos], xp_recv.at[pos], stage=stage + 1)
+    def owner_of(idx):
+        return jnp.where(idx < n_chunk, me, far)
+
+    def act_copy(idx):
+        dst = x_v.at[lax.rem(idx, n_chunk), owner_of(idx)]
+        return remote(yf_v.at[lax.rem(idx, 2)], dst, xp_send.at[idx], xp_recv.at[idx], stage=stage + 1)
 
     def grad_copy(pos):
         return remote(yb_v.at[lax.rem(pos, 2)], e_v.at[pos, me], ep_send.at[pos], ep_recv.at[pos], stage=stage - 1)
 
-    def forward(pos):
+    def forward(idx):
+        pos, owner = lax.rem(idx, n_chunk), owner_of(idx)
+        kept = jnp.where(idx < n_chunk, pos, n_chunk)
+
         @pl.when(not_first)
         def _():
-            act_copy(pos).wait_recv()
-            start_shared(x_gather, pos)
-
-        @pl.when(not_last & (pos >= 2))
-        def _():
-            act_copy(pos - 2).wait_send()
-
-        slot = lax.rem(pos, 2)
+            act_copy(idx).wait_recv()
+            pl.when(idx < n_chunk)(lambda: start_shared(x_gather, pos))
+
+        @pl.when(not_last & (idx >= 2))
+        def _():
+            act_copy(idx - 2).wait_send()
+
+        slot = lax.rem(idx, 2)
         for part in range(n_model):
             cols = pl.ds(part * hid, hid)
-            pre = dot_nn(x_v[pos, me], w1_v[part]).astype(jnp.bfloat16)
-            u_v[pos, :, cols] = pre
+            pre = dot_nn(x_v[pos, owner], w1_v[part]).astype(jnp.bfloat16)
+            u_v[kept, :, cols] = pre
             a_v[:, cols] = gelu_tanh(pre.astype(jnp.float32)).astype(jnp.bfloat16)
         branch = dot_nn(a_v[...], w2_v[...].reshape(n_model * hid, dim))
-        yf_v[slot] = (x_v[pos, me].astype(jnp.float32) + branch).astype(jnp.bfloat16)
+        yf_v[slot] = (x_v[pos, owner].astype(jnp.float32) + branch).astype(jnp.bfloat16)
 
         @pl.when(not_last)
         def _():
-            act_copy(pos).start()
+            act_copy(idx).start()
 
         @pl.when(is_last)
         def _():
@@ -246,7 +255,9 @@
     def weight_grads(pos):
         @pl.when(not_first)
         def _():
-            arrived(x_gather, pos)
+            shared(*x_gather, pos, True).wait_recv()
+            shared(*x_gather, pos, False).wait_recv()
+            pl.when(is_last)(lambda: act_copy(n_chunk + pos).wait_recv())
 
         arrived(e_gather, pos)
         pre = dot_nn(x_v[pos].reshape(rows_all, dim), w1_v[me]).astype(jnp.bfloat16)
@@ -264,26 +275,22 @@
     def loss_down():
         return remote(loss_tot, loss_tot, loss_send.at[3], loss_recv.at[3], stage=stage - 1)
 
-    warm = jnp.minimum(n_chunk, 1 + 3 * (last - stage)) - 1
+    depth = last - stage
+    n_forward = jnp.where(is_last, n_chunk, 2 * n_chunk)
+    warm = jnp.minimum(2 * n_chunk - 1, depth * (depth + 2))
     is_late = stage >= n_stage // 2
-    relay_at = jnp.where(is_late, warm + n_chunk - 2, warm + 1)
-    grads_at = jnp.where(is_late, warm + n_chunk, warm + 2)
+    relay_at = warm + jnp.where(is_late, 5, 1)
+    grads_at = warm + jnp.where(is_late, n_chunk, 2)
     loss_at = jnp.where(is_late, grads_at, grads_at + n_chunk - 2)
-    x_lag = 5
-
-    def due(turn, start, fn):
+
+    def due(turn, start, fn, count=n_chunk):
         pos = turn - start
-        pl.when((pos >= 0) & (pos < n_chunk))(lambda: fn(pos))
+        pl.when((pos >= 0) & (pos < count))(lambda: fn(pos))
 
     @pl.loop(0, grads_at + n_chunk)
     def _(turn):
-        due(turn, 0, forward)
+        due(turn, 0, forward, n_forward)
         due(turn, warm, backward)
-
-        @pl.when(not_first)
-        def _():
-            due(turn, x_lag, functools.partial(relay, x_gather))
-
         due(turn, relay_at, functools.partial(relay, e_gather))
 
         @pl.when(is_last & (turn == n_chunk - 1))
@@ -319,18 +326,19 @@
     def _(pos):
         @pl.when(not_first)
         def _():
-            finish_gather(x_gather, pos)
-
-        finish_gather(e_gather, pos)
-
-    for pos in (n_chunk - 2, n_chunk - 1):
+            finish_shared(x_gather, pos)
+
+        finish_shared(e_gather, pos)
+        finish_passed(e_gather, pos)
+
+    for back in (2, 1):
         @pl.when(not_last)
         def _():
-            act_copy(pos).wait_send()
+            act_copy(2 * n_chunk - back).wait_send()
 
         @pl.when(not_first)
         def _():
-            grad_copy(pos).wait_send()
+            grad_copy(n_chunk - back).wait_send()
 
     @pl.when(not_first)
     def _():
@@ -371,7 +379,7 @@
                 pltpu.VMEM((n_chunk, n_model, CHUNK, dim), bf16),
                 pltpu.VMEM((2, CHUNK, dim), bf16),
                 pltpu.VMEM((2, CHUNK, dim), bf16),
-                pltpu.VMEM((n_chunk, CHUNK, n_model * hid), bf16),
+                pltpu.VMEM((n_chunk + 1, CHUNK, n_model * hid), bf16),
                 pltpu.VMEM((CHUNK, n_model * hid), bf16),
                 pltpu.VMEM((n_model * CHUNK, hid), bf16),
                 pltpu.VMEM((n_model * CHUNK, hid), bf16),
@@ -379,8 +387,8 @@
                 pltpu.VMEM((4, 8, 128), f32),
                 pltpu.VMEM((8, 128), f32),
                 dma((2 + n_model,)), dma((2, 6)), dma((2, 6)),
-                dma((n_chunk,)), dma((n_chunk,)), dma((n_chunk,)), dma((n_chunk,)),
-                dma((3, n_chunk)), dma((3, n_chunk)), dma((3, n_chunk)), dma((3, n_chunk)),
+                dma((2 * n_chunk,)), dma((2 * n_chunk,)), dma((n_chunk,)), dma((n_chunk,)),
+                dma((2, n_chunk)), dma((2, n_chunk)), dma((3, n_chunk)), dma((3, n_chunk)),
                 dma((4,)), dma((4,)),
             ],
             compiler_params=pltpu.CompilerParams(

time: 375 us -> 371 us (0.989); the launches traced: 371 us -> 371 us
  no operation moved by 1% of the time
where the time goes in v3:
time: 371 us
  Pallas kernels  362 us (98%)
  local copies, waits for them, and re-layouts  8.15 us (2%)
    pallas_call x1, Pallas kernels, stage_step(): pl.pallas_call(functools.partial(step_kernel, n_stage, n_model, n_chunk,...  362 us

profile of v3, /device:TPU:102, one launch (start us, length us, event | category | flops | bytes accessed | tf_op | source)
XLA Modules:
  0.0 371.2 jit_solution(9800812898066183037)
XLA Ops:
  0.6 362.4 %shard_map.67 = (f32[1024,1024]{1,0:T(8,128)}, f32[1024,1024]{1,0:T(8,128)}, f32[8,128]{1,0:T(8,128)}) custom-call(bf16[4,9,128,1024]{3,2,1,0:T(8,128)(2,1)} %bitcast.7, bf16[4,9,128,1024]{3,2,1,0:T(8,128)(2,1)} %bitcast.8, bf16[1024,1024]{1,0:T(8,128)(2,1)} %bitcast.11, bf16[1024,1024]{1,0:T(8,128)(2,1)} %bitcast.12), custom_call_target="tpu_custom_call" | custom-call | tf_op jit(solution)/shard_map/pallas_call | solution.py:366
  363.1 1.2 slice.3
  364.3 0.0 copy-start
  364.3 4.9 %copy.9 = f32[1,1,1024,1024]{3,2,1,0:T(8,128)} copy(f32[1,1,1024,1024]{3,2,1,0:T(8,128)} %bitcast.10) | data formatting | bytes 8388608
  369.2 0.0 copy-done
  369.2 2.0 copy.10
Async XLA Ops:
  364.3 4.9 %copy-start = (f32[1024,1024]{1,0:T(8,128)S(1)}, f32[1024,1024]{1,0:T(8,128)}, u32[]{:S(2)}) copy-start(f32[1024,1024]{1,0:T(8,128)} %get-tuple-element.7) | copy-start | bytes 12582916

commit v4 on v3

--- a/solution.py
+++ b/solution.py
@@ -366,8 +366,8 @@
         dw1, dw2, loss = pl.pallas_call(
             functools.partial(step_kernel, n_stage, n_model, n_chunk, grad_scale),
             out_shape=(
-                jax.ShapeDtypeStruct((dim, hid), f32),
-                jax.ShapeDtypeStruct((hid, dim), f32),
+                pltpu.VMEM((dim, hid), f32),
+                pltpu.VMEM((hid, dim), f32),
                 jax.ShapeDtypeStruct((8, 128), f32),
             ),
             in_specs=[any_spec] * 4,
@@ -392,7 +392,7 @@
                 dma((4,)), dma((4,)),
             ],
             compiler_params=pltpu.CompilerParams(
-                collective_id=0, has_side_effects=True, vmem_limit_bytes=67043328
+                collective_id=0, has_side_effects=True, vmem_limit_bytes=58000000
             ),
         )(inputs.reshape(by_owner), targets.reshape(by_owner), w1, w2)
         return dw1[None, None], dw2[None, None], loss[0, :1]

time: 371 us -> 366 us (0.987)
  no operation moved by 1% of the time
where the time goes in v4:
time: 366 us
  Pallas kernels  361 us (99%)
  local copies, waits for them, and re-layouts  5.21 us (1%)
    pallas_call x1, Pallas kernels, stage_step(): pl.pallas_call(functools.partial(step_kernel, n_stage, n_model, n_chunk,...  361 us

profile of v4, /device:TPU:102, one launch (start us, length us, event | category | flops | bytes accessed | tf_op | source)
XLA Modules:
  0.0 366.4 jit_solution(13929976306378590476)
XLA Ops:
  0.6 360.5 %shard_map.67 = (f32[1024,1024]{1,0:T(8,128)S(1)}, f32[1024,1024]{1,0:T(8,128)S(1)}, f32[8,128]{1,0:T(8,128)}) custom-call(bf16[4,9,128,1024]{3,2,1,0:T(8,128)(2,1)} %bitcast.9, bf16[4,9,128,1024]{3,2,1,0:T(8,128)(2,1)} %bitcast.10, bf16[1024,1024]{1,0:T(8,128)(2,1)} %bitcast.11, bf16[1024,1024]{1,0:T(8,128)(2,1)} %bitcast.12), custom_call_target="tpu_custom_call" | custom-call | tf_op jit(solution)/shard_map/pallas_call | solution.py:366
  361.2 1.2 slice.3
  362.3 2.0 copy.9
  364.4 2.0 copy.10
